TPU v7x, 32 devices: a whole 2x2x4 slice. The times are simulated.
32 devices in a mesh: blk: 16 (over z, y, core), head: 2 (over x).
Axes of the slice: x: 2, y: 2, z: 4, core: 2. Of those that a mesh axis runs over, the one named last changes fastest.
Arguments:
- query: bfloat16 [4096, 4096], P(('blk', 'head')), may hold values from -6 to 6
- key: bfloat16 [4096, 1024], P(('blk', 'head')), may hold values from -6 to 6
- value: bfloat16 [4096, 1024], P(('blk', 'head')), may hold values from -6 to 6
- grad_out: bfloat16 [4096, 4096], P(('blk', 'head')), may hold values from -6 to 6
- doc_lengths: int32 [32], replicated, may hold values from 1 to 256, 4096 in all
Outputs:
- attended: bfloat16 [4096, 4096], P(('blk', 'head'))
- grad_query: bfloat16 [4096, 4096], P(('blk', 'head'))
- grad_key: bfloat16 [4096, 1024], P(('blk', 'head'))
- grad_value: bfloat16 [4096, 1024], P(('blk', 'head'))
Inputs may be any that keep to these rules, and one draw needn't show every extreme that they name: `doc_lengths`: every document has at most 256 tokens, one has exactly 256, and the lengths sum to 4096.
All inputs are finite; a program needn't handle non-finite values.
Results may differ from a plain program's by a relative error of at most 0.0088.
Values may be sent and summed in bfloat16 or wider, within the bound.
A program may use at most 128 MiB of HBM per device.

v0:
```python
import functools
import math

import jax
import jax.numpy as jnp
from jax import lax
from jax.experimental import pallas as pl
from jax.experimental.pallas import tpu as pltpu
from jax.sharding import PartitionSpec as P

HEAD_DIM = 128
EXCLUDED = -1e30
MESH = pl.DeviceIdType.MESH


def kernel(
    back, total, lens, q_hbm, k_hbm, v_hbm, do_hbm, attbuf, dqbuf, dkbuf, dvbuf,
    window, qbuf, dobuf, part, landed, own, bias,
    kv_in, q_in, kv_send, kv_recv, g_send, g_recv,
):
    rows = q_hbm.shape[0]
    kv_heads = k_hbm.shape[1] // HEAD_DIM
    groups = q_hbm.shape[1] // k_hbm.shape[1]
    width = groups * HEAD_DIM
    span = (back + 1) * rows
    scaling = HEAD_DIM ** (-0.5)
    me = lax.axis_index("blk") * back + lax.axis_index("head")

    def device(number):
        return {"blk": number // back, "head": number % back}

    def columns(g, size):
        return pl.ds(pl.multiple_of(g * size, size), size)

    def slot(k):
        return pl.ds((back - k) * rows, rows)

    def kv_load(g, which):
        return pltpu.make_async_copy(
            (k_hbm, v_hbm)[which].at[:, columns(g, HEAD_DIM)],
            window.at[g, which, slot(0), :],
            kv_in.at[which, g],
        )

    def q_load(g, which):
        return pltpu.make_async_copy(
            (q_hbm, do_hbm)[which].at[:, columns(g, width)],
            (qbuf, dobuf)[which].at[g],
            q_in.at[which, g],
        )

    def kv_copy(g, k):
        return pltpu.make_async_remote_copy(
            src_ref=window.at[g, :, slot(0), :],
            dst_ref=window.at[g, :, slot(k), :],
            send_sem=kv_send.at[k - 1, g],
            recv_sem=kv_recv.at[k - 1, g],
            device_id=device(me + k),
            device_id_type=MESH,
        )

    def g_copy(g, k):
        return pltpu.make_async_remote_copy(
            src_ref=part.at[g, :, slot(k), :],
            dst_ref=landed.at[g, k - 1],
            send_sem=g_send.at[k - 1, g],
            recv_sem=g_recv.at[k - 1, g],
            device_id=device(me - k),
            device_id_type=MESH,
        )

    @pl.loop(0, kv_heads)
    def _(g):
        kv_load(g, 0).start()
        kv_load(g, 1).start()

    barrier = pltpu.get_barrier_semaphore()
    for k in range(1, back + 1):
        @pl.when(me - k >= 0)
        def _():
            pl.semaphore_signal(barrier, inc=1, device_id=device(me - k), device_id_type=MESH)

    @pl.loop(0, kv_heads)
    def _(g):
        q_load(g, 0).start()
        q_load(g, 1).start()

    @pl.when(me < total - 1)
    def _():
        pl.semaphore_wait(barrier, jnp.minimum(total - 1 - me, back))

    @pl.loop(0, kv_heads)
    def _(g):
        kv_load(g, 0).wait()
        kv_load(g, 1).wait()
        for k in range(1, back + 1):
            @pl.when(me + k < total)
            def _():
                kv_copy(g, k).start()

    for k in range(1, back + 1):
        @pl.when(me - k < 0)
        def _():
            window[:, :, slot(k), :] = jnp.zeros((kv_heads, 2, rows, HEAD_DIM), jnp.bfloat16)

        @pl.when(me + k >= total)
        def _():
            landed[:, k - 1] = jnp.zeros((kv_heads, 2, rows, HEAD_DIM), jnp.bfloat16)

    query_pos = me * rows + lax.broadcasted_iota(jnp.int32, (1, rows), 1)

    def latest(d, carry):
        start, first = carry
        return start + lens[d], jnp.where(query_pos >= start, start, first)

    _, first = lax.fori_loop(
        0, lens.shape[0], latest, (jnp.int32(0), jnp.zeros((1, rows), jnp.int32))
    )
    key_pos = (me - back) * rows + lax.broadcasted_iota(jnp.int32, (span, rows), 0)
    bias[...] = jnp.where((key_pos <= query_pos) & (key_pos >= first), 0.0, EXCLUDED)

    def dot(a, b, a_dim, b_dim):
        return lax.dot_general(
            a, b, (((a_dim,), (b_dim,)), ((), ())), preferred_element_type=jnp.float32
        )

    def stacked(values):
        return jnp.concatenate(
            [values[:, h * HEAD_DIM : (h + 1) * HEAD_DIM] for h in range(groups)], axis=0
        )

    @pl.loop(0, kv_heads)
    def _(g):
        q_load(g, 0).wait()
        q_load(g, 1).wait()
        for k in range(1, back + 1):
            @pl.when(me - k >= 0)
            def _():
                kv_copy(g, k).wait_recv()

        keys, values = window[g, 0], window[g, 1]
        queries, grads = stacked(qbuf[g]), stacked(dobuf[g])
        kept = jnp.concatenate([bias[...]] * groups, axis=1)
        scores = dot(keys, queries, 1, 1) * (scaling * math.log2(math.e)) + kept
        peak = jnp.max(scores, axis=0, keepdims=True)
        raised = jnp.exp2(scores - peak)
        weights = raised * (1.0 / jnp.sum(raised, axis=0, keepdims=True))
        weights_bf = weights.astype(jnp.bfloat16)
        attended = dot(values, weights_bf, 0, 0)
        grad_weights = dot(values, grads, 1, 1)
        delta = jnp.sum(weights * grad_weights, axis=0, keepdims=True)
        grad_scores = (weights * (grad_weights - delta)).astype(jnp.bfloat16)
        grad_query = dot(keys, grad_scores, 0, 0) * scaling
        grad_key = dot(grad_scores, queries, 1, 0) * scaling
        grad_value = dot(weights_bf, grads, 1, 0)
        part[g, 0] = grad_key[: back * rows].astype(jnp.bfloat16)
        part[g, 1] = grad_value[: back * rows].astype(jnp.bfloat16)
        own[g, 0] = grad_key[back * rows :]
        own[g, 1] = grad_value[back * rows :]
        for h in range(groups):
            at = slice(h * HEAD_DIM, (h + 1) * HEAD_DIM)
            to = columns(g * groups + h, HEAD_DIM)
            attbuf[:, to] = attended[:, at].T.astype(jnp.bfloat16)
            dqbuf[:, to] = grad_query[:, at].T.astype(jnp.bfloat16)
        for k in range(1, back + 1):
            @pl.when(me - k >= 0)
            def _():
                g_copy(g, k).start()

    @pl.loop(0, kv_heads)
    def _(g):
        for k in range(1, back + 1):
            @pl.when(me + k < total)
            def _():
                g_copy(g, k).wait_recv()
        sums = own[g]
        for k in range(1, back + 1):
            sums = sums + landed[g, k - 1].astype(jnp.float32)
        dkbuf[:, columns(g, HEAD_DIM)] = sums[0].astype(jnp.bfloat16)
        dvbuf[:, columns(g, HEAD_DIM)] = sums[1].astype(jnp.bfloat16)

    @pl.loop(0, kv_heads)
    def _(g):
        for k in range(1, back + 1):
            @pl.when(me + k < total)
            def _():
                kv_copy(g, k).wait_send()

            @pl.when(me - k >= 0)
            def _():
                g_copy(g, k).wait_send()


def write_out(att, dq, dk, dv, att_hbm, dq_hbm, dk_hbm, dv_hbm, sems):
    copies = []
    pairs = ((att, att_hbm), (dq, dq_hbm), (dk, dk_hbm), (dv, dv_hbm))
    for which, (source, target) in enumerate(pairs):
        step = source.shape[0] // sems.shape[1]
        for piece in range(sems.shape[1]):
            at = slice(piece * step, (piece + 1) * step)
            copies.append(
                pltpu.make_async_copy(source.at[at], target.at[at], sems.at[which, piece])
            )
    for copy in copies:
        copy.start()
    for copy in copies:
        copy.wait()


def solution(mesh):
    back = mesh.shape["head"]
    total = mesh.shape["blk"] * back

    def per_device(query, key, value, grad_out, doc_lengths):
        rows, kv_heads = query.shape[0], key.shape[1] // HEAD_DIM
        width = query.shape[1] // kv_heads
        bf, f32 = jnp.bfloat16, jnp.float32
        anywhere = pl.BlockSpec(memory_space=pl.ANY)
        dma = pltpu.SemaphoreType.DMA
        results = pl.pallas_call(
            functools.partial(kernel, back, total),
            out_shape=[
                pltpu.VMEM(query.shape, bf),
                pltpu.VMEM(query.shape, bf),
                pltpu.VMEM(key.shape, bf),
                pltpu.VMEM(key.shape, bf),
            ],
            in_specs=[pl.BlockSpec(memory_space=pltpu.SMEM)] + [anywhere] * 4,
            out_specs=[pl.BlockSpec(memory_space=pltpu.VMEM)] * 4,
            scratch_shapes=[
                pltpu.VMEM((kv_heads, 2, (back + 1) * rows, HEAD_DIM), bf),
                pltpu.VMEM((kv_heads, rows, width), bf),
                pltpu.VMEM((kv_heads, rows, width), bf),
                pltpu.VMEM((kv_heads, 2, back * rows, HEAD_DIM), bf),
                pltpu.VMEM((kv_heads, back, 2, rows, HEAD_DIM), bf),
                pltpu.VMEM((kv_heads, 2, rows, HEAD_DIM), f32),
                pltpu.VMEM(((back + 1) * rows, rows), f32),
                dma((2, kv_heads)),
                dma((2, kv_heads)),
                dma((back, kv_heads)),
                dma((back, kv_heads)),
                dma((back, kv_heads)),
                dma((back, kv_heads)),
            ],
            compiler_params=pltpu.CompilerParams(collective_id=0, has_side_effects=True),
        )(doc_lengths, query, key, value, grad_out)
        results = [pltpu.with_memory_space_constraint(r, pltpu.VMEM) for r in results]
        return pl.pallas_call(
            write_out,
            out_shape=[
                jax.ShapeDtypeStruct(query.shape, bf),
                jax.ShapeDtypeStruct(query.shape, bf),
                jax.ShapeDtypeStruct(key.shape, bf),
                jax.ShapeDtypeStruct(key.shape, bf),
            ],
            in_specs=[pl.BlockSpec(memory_space=pltpu.VMEM)] * 4,
            out_specs=[anywhere] * 4,
            scratch_shapes=[dma((4, 4))],
        )(*results)

    split = P(("blk", "head"), None)
    return jax.shard_map(
        per_device,
        mesh=mesh,
        in_specs=(split, split, split, split, P()),
        out_specs=(split, split, split, split),
        check_vma=False,
    )
```

profile of v0, /device:TPU:0, one launch (start us, length us, event | category | flops | bytes accessed | tf_op | source)
XLA Modules:
  0.0 31.4 jit_solution(12154878510168784728)
XLA Ops:
  0.6 29.1 %shard_map.84 = (bf16[128,4096]{1,0:T(8,128)(2,1)S(1)}, bf16[128,4096]{1,0:T(8,128)(2,1)S(1)}, bf16[128,1024]{1,0:T(8,128)(2,1)S(1)}, bf16[128,1024]{1,0:T(8,128)(2,1)S(1)}) custom-call(s32[32]{0:T(128)} %lens.1, bf16[128,4096]{1,0:T(8,128)(2,1)} %q_hbm.1, bf16[128,1024]{1,0:T(8,128)(2,1)} %k_hbm.1, bf16[128,1024]{1,0:T(8,128)(2,1)} %v_hbm.1, ...), custom_call_target="tpu_custom_call" | custom-call | tf_op jit(solution)/shard_map/pallas_call | solution.py:220
  29.8 1.6 %shard_map.85 = (bf16[128,4096]{1,0:T(8,128)(2,1)}, bf16[128,4096]{1,0:T(8,128)(2,1)}, bf16[128,1024]{1,0:T(8,128)(2,1)}, bf16[128,1024]{1,0:T(8,128)(2,1)}) custom-call(bf16[128,4096]{1,0:T(8,128)(2,1)S(1)} %get-tuple-element.8.att, bf16[128,4096]{1,0:T(8,128)(2,1)S(1)} %get-tuple-element.9.dq, bf16[128,1024]{1,0:T(8,128)(2,1)S(1)} %get-tuple-element.10.dk, ...), custom_call_target="tpu_custom_call" | custom-call | tf_op jit(solution)/shard_map/pallas_call | solution.py:248
where the time goes:
time: 31.5 us; the launch traced here: 31.4 us
  Pallas kernels  30.7 us (97%)
  between operations  0.64 us (2%)
    pallas_call x1, Pallas kernels, per_device(): pl.pallas_call(functools.partial(kernel, back, total), out_shape=[pltpu.V...  29.1 us
    pallas_call x1, Pallas kernels, per_device(): pl.pallas_call(write_out, out_shape=[jax.ShapeDtypeStruct(query.shape, bf...  1.61 us

commit v1 on v0

v1 whole, which is shorter than its diff:
```python
import functools
import math

import jax
import jax.numpy as jnp
from jax import lax
from jax.experimental import pallas as pl
from jax.experimental.pallas import tpu as pltpu
from jax.sharding import PartitionSpec as P

HEAD_DIM = 128
EXCLUDED = -1e30
HEADS_A_COPY = 2
MESH = pl.DeviceIdType.MESH


def kernel(
    back, total, lens_hbm, q_hbm, k_hbm, v_hbm, do_hbm, attbuf, dqbuf, dkbuf, dvbuf,
    window, qbuf, dobuf, part, landed, own, bias, lens,
    lens_in, kv_in, q_in, kv_send, kv_recv, g_send, g_recv,
):
    rows = q_hbm.shape[0]
    kv_heads = k_hbm.shape[1] // HEAD_DIM
    groups = q_hbm.shape[1] // k_hbm.shape[1]
    width = groups * HEAD_DIM
    span = (back + 1) * rows
    scaling = HEAD_DIM ** (-0.5)
    chunks = kv_send.shape[1]
    per = kv_heads // chunks
    me = lax.axis_index("blk") * back + lax.axis_index("head")

    def device(number):
        return {"blk": number // back, "head": number % back}

    def columns(g, size):
        return pl.ds(pl.multiple_of(g * size, size), size)

    def heads(c):
        return pl.ds(c * per, per)

    def kv_load(g, which):
        return pltpu.make_async_copy(
            (k_hbm, v_hbm)[which].at[:, columns(g, HEAD_DIM)],
            window.at[0, g, which],
            kv_in.at[which, g],
        )

    def q_load(g, which):
        return pltpu.make_async_copy(
            (q_hbm, do_hbm)[which].at[:, columns(g, width)],
            (qbuf, dobuf)[which].at[g],
            q_in.at[which, g],
        )

    def kv_copy(c, k):
        return pltpu.make_async_remote_copy(
            src_ref=window.at[0, heads(c)],
            dst_ref=window.at[k, heads(c)],
            send_sem=kv_send.at[k - 1, c],
            recv_sem=kv_recv.at[k - 1, c],
            device_id=device(me + k),
            device_id_type=MESH,
        )

    def g_copy(c, k):
        return pltpu.make_async_remote_copy(
            src_ref=part.at[k - 1, heads(c)],
            dst_ref=landed.at[k - 1, heads(c)],
            send_sem=g_send.at[k - 1, c],
            recv_sem=g_recv.at[k - 1, c],
            device_id=device(me - k),
            device_id_type=MESH,
        )

    barrier = pltpu.get_barrier_semaphore()
    for k in range(1, back + 1):
        @pl.when(me - k >= 0)
        def _():
            pl.semaphore_signal(barrier, inc=1, device_id=device(me - k), device_id_type=MESH)

    @pl.loop(0, kv_heads)
    def _(g):
        kv_load(g, 0).start()
        kv_load(g, 1).start()

    lens_load = pltpu.make_async_copy(lens_hbm, lens, lens_in)
    lens_load.start()

    @pl.loop(0, kv_heads)
    def _(g):
        q_load(g, 0).start()
        q_load(g, 1).start()

    @pl.when(me < total - 1)
    def _():
        pl.semaphore_wait(barrier, jnp.minimum(total - 1 - me, back))

    @pl.loop(0, chunks)
    def _(c):
        for i in range(per):
            kv_load(c * per + i, 0).wait()
            kv_load(c * per + i, 1).wait()
        for k in range(1, back + 1):
            @pl.when(me + k < total)
            def _():
                kv_copy(c, k).start()

    for k in range(1, back + 1):
        @pl.when(me - k < 0)
        def _():
            window[k] = jnp.zeros((kv_heads, 2, rows, HEAD_DIM), jnp.bfloat16)

        @pl.when(me + k >= total)
        def _():
            landed[k - 1] = jnp.zeros((kv_heads, 2, rows, HEAD_DIM), jnp.bfloat16)

    lens_load.wait()
    query_pos = me * rows + lax.broadcasted_iota(jnp.int32, (1, rows), 1)

    def latest(d, carry):
        start, first = carry
        return start + lens[d], jnp.where(query_pos >= start, start, first)

    _, first = lax.fori_loop(
        0, lens.shape[0], latest, (jnp.int32(0), jnp.zeros((1, rows), jnp.int32))
    )
    key_pos = (me - back) * rows + lax.broadcasted_iota(jnp.int32, (span, rows), 0)
    bias[...] = jnp.where((key_pos <= query_pos) & (key_pos >= first), 0.0, EXCLUDED)

    def dot(a, b, a_dim, b_dim):
        return lax.dot_general(
            a, b, (((a_dim,), (b_dim,)), ((), ())), preferred_element_type=jnp.float32
        )

    def stacked(values):
        return jnp.concatenate(
            [values[:, h * HEAD_DIM : (h + 1) * HEAD_DIM] for h in range(groups)], axis=0
        )

    @pl.loop(0, kv_heads)
    def _(g):
        q_load(g, 0).wait()
        q_load(g, 1).wait()

        @pl.when(g % per == 0)
        def _():
            for k in range(1, back + 1):
                @pl.when(me - k >= 0)
                def _():
                    kv_copy(g // per, k).wait_recv()

        keys, values = (
            jnp.concatenate([window[k, g, which] for k in range(back, -1, -1)], axis=0)
            for which in range(2)
        )
        queries, grads = stacked(qbuf[g]), stacked(dobuf[g])
        kept = jnp.concatenate([bias[...]] * groups, axis=1)
        scores = dot(keys, queries, 1, 1) * (scaling * math.log2(math.e)) + kept
        peak = jnp.max(scores, axis=0, keepdims=True)
        raised = jnp.exp2(scores - peak)
        weights = raised * (1.0 / jnp.sum(raised, axis=0, keepdims=True))
        weights_bf = weights.astype(jnp.bfloat16)
        attended = dot(values, weights_bf, 0, 0)
        grad_weights = dot(values, grads, 1, 1)
        delta = jnp.sum(weights * grad_weights, axis=0, keepdims=True)
        grad_scores = (weights * (grad_weights - delta)).astype(jnp.bfloat16)
        grad_query = dot(keys, grad_scores, 0, 0) * scaling
        grad_key = dot(grad_scores, queries, 1, 0) * scaling
        grad_value = dot(weights_bf, grads, 1, 0)
        for k in range(1, back + 1):
            at = slice((back - k) * rows, (back - k + 1) * rows)
            part[k - 1, g, 0] = grad_key[at].astype(jnp.bfloat16)
            part[k - 1, g, 1] = grad_value[at].astype(jnp.bfloat16)
        own[g, 0] = grad_key[back * rows :]
        own[g, 1] = grad_value[back * rows :]

        @pl.when(g % per == per - 1)
        def _():
            for k in range(1, back + 1):
                @pl.when(me - k >= 0)
                def _():
                    g_copy(g // per, k).start()

        for h in range(groups):
            at = slice(h * HEAD_DIM, (h + 1) * HEAD_DIM)
            to = columns(g * groups + h, HEAD_DIM)
            attbuf[:, to] = attended[:, at].T.astype(jnp.bfloat16)
            dqbuf[:, to] = grad_query[:, at].T.astype(jnp.bfloat16)

    @pl.loop(0, chunks)
    def _(c):
        for k in range(1, back + 1):
            @pl.when(me + k < total)
            def _():
                g_copy(c, k).wait_recv()
        for i in range(per):
            g = c * per + i
            sums = own[g]
            for k in range(1, back + 1):
                sums = sums + landed[k - 1, g].astype(jnp.float32)
            dkbuf[:, columns(g, HEAD_DIM)] = sums[0].astype(jnp.bfloat16)
            dvbuf[:, columns(g, HEAD_DIM)] = sums[1].astype(jnp.bfloat16)

    @pl.loop(0, chunks)
    def _(c):
        for k in range(1, back + 1):
            @pl.when(me + k < total)
            def _():
                kv_copy(c, k).wait_send()

            @pl.when(me - k >= 0)
            def _():
                g_copy(c, k).wait_send()


def write_out(att, dq, dk, dv, att_hbm, dq_hbm, dk_hbm, dv_hbm, sems):
    pairs = ((att, att_hbm), (dq, dq_hbm), (dk, dk_hbm), (dv, dv_hbm))
    copies = [
        pltpu.make_async_copy(source, target, sems.at[which])
        for which, (source, target) in enumerate(pairs)
    ]
    for copy in copies:
        copy.start()
    for copy in copies:
        copy.wait()


def solution(mesh):
    back = mesh.shape["head"]
    total = mesh.shape["blk"] * back

    def per_device(query, key, value, grad_out, doc_lengths):
        rows, kv_heads = query.shape[0], key.shape[1] // HEAD_DIM
        width = query.shape[1] // kv_heads
        chunks = kv_heads // math.gcd(kv_heads, HEADS_A_COPY)
        bf, f32 = jnp.bfloat16, jnp.float32
        anywhere = pl.BlockSpec(memory_space=pl.ANY)
        dma = pltpu.SemaphoreType.DMA
        results = pl.pallas_call(
            functools.partial(kernel, back, total),
            out_shape=[
                pltpu.VMEM(query.shape, bf),
                pltpu.VMEM(query.shape, bf),
                pltpu.VMEM(key.shape, bf),
                pltpu.VMEM(key.shape, bf),
            ],
            in_specs=[anywhere] * 5,
            out_specs=[pl.BlockSpec(memory_space=pltpu.VMEM)] * 4,
            scratch_shapes=[
                pltpu.VMEM((back + 1, kv_heads, 2, rows, HEAD_DIM), bf),
                pltpu.VMEM((kv_heads, rows, width), bf),
                pltpu.VMEM((kv_heads, rows, width), bf),
                pltpu.VMEM((back, kv_heads, 2, rows, HEAD_DIM), bf),
                pltpu.VMEM((back, kv_heads, 2, rows, HEAD_DIM), bf),
                pltpu.VMEM((kv_heads, 2, rows, HEAD_DIM), f32),
                pltpu.VMEM(((back + 1) * rows, rows), f32),
                pltpu.SMEM(doc_lengths.shape, jnp.int32),
                dma,
                dma((2, kv_heads)),
                dma((2, kv_heads)),
                dma((back, chunks)),
                dma((back, chunks)),
                dma((back, chunks)),
                dma((back, chunks)),
            ],
            compiler_params=pltpu.CompilerParams(collective_id=0, has_side_effects=True),
        )(doc_lengths, query, key, value, grad_out)
        results = [pltpu.with_memory_space_constraint(r, pltpu.VMEM) for r in results]
        return pl.pallas_call(
            write_out,
            out_shape=[
                jax.ShapeDtypeStruct(query.shape, bf),
                jax.ShapeDtypeStruct(query.shape, bf),
                jax.ShapeDtypeStruct(key.shape, bf),
                jax.ShapeDtypeStruct(key.shape, bf),
            ],
            in_specs=[pl.BlockSpec(memory_space=pltpu.VMEM)] * 4,
            out_specs=[anywhere] * 4,
            scratch_shapes=[dma((4,))],
        )(*results)

    split = P(("blk", "head"), None)
    return jax.shard_map(
        per_device,
        mesh=mesh,
        in_specs=(split, split, split, split, P()),
        out_specs=(split, split, split, split),
        check_vma=False,
    )
```

time: 31.5 us -> 30.7 us (0.975)
  Pallas kernels: 30.7 us -> 29.9 us
    pallas_call x1, Pallas kernels: 29.1 us -> 28.4 us  [per_device(): pl.pallas_call(functools.partial(kernel, back, total), out_shape=[pltpu.V...]
where the time goes in v1:
time: 30.7 us; the launch traced here: 30.5 us
  Pallas kernels  29.9 us (97%)
  between operations  0.64 us (2%)
    pallas_call x1, Pallas kernels, per_device(): pl.pallas_call(functools.partial(kernel, back, total), out_shape=[pltpu.V...  28.4 us
    pallas_call x1, Pallas kernels, per_device(): pl.pallas_call(write_out, out_shape=[jax.ShapeDtypeStruct(query.shape, bf...  1.52 us

profile of v1, /device:TPU:0, one launch (start us, length us, event | category | flops | bytes accessed | tf_op | source)
XLA Modules:
  0.0 30.5 jit_solution(11929754192803942816)
XLA Ops:
  0.6 28.4 %shard_map.84 = (bf16[128,4096]{1,0:T(8,128)(2,1)S(1)}, bf16[128,4096]{1,0:T(8,128)(2,1)S(1)}, bf16[128,1024]{1,0:T(8,128)(2,1)S(1)}, bf16[128,1024]{1,0:T(8,128)(2,1)S(1)}) custom-call(s32[32]{0:T(128)} %lens_hbm.1, bf16[128,4096]{1,0:T(8,128)(2,1)} %q_hbm.1, bf16[128,1024]{1,0:T(8,128)(2,1)} %k_hbm.1, bf16[128,1024]{1,0:T(8,128)(2,1)} %v_hbm.1, ...), custom_call_target="tpu_custom_call" | custom-call | tf_op jit(solution)/shard_map/pallas_call | solution.py:239
  29.0 1.5 %shard_map.85 = (bf16[128,4096]{1,0:T(8,128)(2,1)}, bf16[128,4096]{1,0:T(8,128)(2,1)}, bf16[128,1024]{1,0:T(8,128)(2,1)}, bf16[128,1024]{1,0:T(8,128)(2,1)}) custom-call(bf16[128,4096]{1,0:T(8,128)(2,1)S(1)} %get-tuple-element.8.att, bf16[128,4096]{1,0:T(8,128)(2,1)S(1)} %get-tuple-element.9.dq, bf16[128,1024]{1,0:T(8,128)(2,1)S(1)} %get-tuple-element.10.dk, ...), custom_call_target="tpu_custom_call" | custom-call | tf_op jit(solution)/shard_map/pallas_call | solution.py:269

commit v2 on v1

--- a/solution.py
+++ b/solution.py
@@ -17,7 +17,7 @@
 def kernel(
     back, total, lens_hbm, q_hbm, k_hbm, v_hbm, do_hbm, attbuf, dqbuf, dkbuf, dvbuf,
     window, qbuf, dobuf, part, landed, own, bias, lens,
-    lens_in, kv_in, q_in, kv_send, kv_recv, g_send, g_recv,
+    lens_in, kv_in, q_in, kv_send, kv_recv, relay_send, g_send, g_recv,
 ):
     rows = q_hbm.shape[0]
     kv_heads = k_hbm.shape[1] // HEAD_DIM
@@ -27,7 +27,11 @@
     scaling = HEAD_DIM ** (-0.5)
     chunks = kv_send.shape[1]
     per = kv_heads // chunks
+    last = chunks - 1
     me = lax.axis_index("blk") * back + lax.axis_index("head")
+    place = me % (2 * back)
+    edge = (place == 2 * back - 1) & (me + back < total) & (back == 2)
+    relays = (place == 1) & (me > back) & (back == 2)
 
     def device(number):
         return {"blk": number // back, "head": number % back}
@@ -62,6 +66,16 @@
             device_id_type=MESH,
         )
 
+    def relay():
+        return pltpu.make_async_remote_copy(
+            src_ref=window.at[back, heads(last)],
+            dst_ref=window.at[1, heads(last)],
+            send_sem=relay_send,
+            recv_sem=kv_recv.at[0, last],
+            device_id=device(me - 1),
+            device_id_type=MESH,
+        )
+
     def g_copy(c, k):
         return pltpu.make_async_remote_copy(
             src_ref=part.at[k - 1, heads(c)],
@@ -95,11 +109,19 @@
     def _():
         pl.semaphore_wait(barrier, jnp.minimum(total - 1 - me, back))
 
-    @pl.loop(0, chunks)
-    def _(c):
+    def kv_loaded(c):
         for i in range(per):
             kv_load(c * per + i, 0).wait()
             kv_load(c * per + i, 1).wait()
+
+    @pl.when(edge)
+    def _():
+        kv_loaded(last)
+        kv_copy(last, back).start()
+
+    @pl.loop(0, chunks - edge.astype(jnp.int32))
+    def _(c):
+        kv_loaded(c)
         for k in range(1, back + 1):
             @pl.when(me + k < total)
             def _():
@@ -145,9 +167,15 @@
         @pl.when(g % per == 0)
         def _():
             for k in range(1, back + 1):
-                @pl.when(me - k >= 0)
+                early = relays & (g // per == last) if k == back else False
+                @pl.when((me - k >= 0) & jnp.logical_not(early))
                 def _():
                     kv_copy(g // per, k).wait_recv()
+
+        @pl.when(relays & (g == 0))
+        def _():
+            kv_copy(last, back).wait_recv()
+            relay().start()
 
         keys, values = (
             jnp.concatenate([window[k, g, which] for k in range(back, -1, -1)], axis=0)
@@ -201,10 +229,15 @@
             dkbuf[:, columns(g, HEAD_DIM)] = sums[0].astype(jnp.bfloat16)
             dvbuf[:, columns(g, HEAD_DIM)] = sums[1].astype(jnp.bfloat16)
 
+    @pl.when(relays)
+    def _():
+        relay().wait_send()
+
     @pl.loop(0, chunks)
     def _(c):
         for k in range(1, back + 1):
-            @pl.when(me + k < total)
+            direct = jnp.logical_not(edge & (c == last)) if k == 1 else True
+            @pl.when((me + k < total) & direct)
             def _():
                 kv_copy(c, k).wait_send()
 
@@ -260,6 +293,7 @@
                 dma((2, kv_heads)),
                 dma((back, chunks)),
                 dma((back, chunks)),
+                dma,
                 dma((back, chunks)),
                 dma((back, chunks)),
             ],

time: 30.7 us -> 29.5 us (0.961)
  Pallas kernels: 29.9 us -> 28.6 us
    pallas_call x1, Pallas kernels: 28.4 us -> 27.1 us  [per_device(): pl.pallas_call(functools.partial(kernel, back, total), out_shape=[pltpu.V...]
where the time goes in v2:
time: 29.5 us; the launch traced here: 29.3 us
  Pallas kernels  28.6 us (97%)
  between operations  0.64 us (2%)
    pallas_call x1, Pallas kernels, per_device(): pl.pallas_call(functools.partial(kernel, back, total), out_shape=[pltpu.V...  27.1 us
    pallas_call x1, Pallas kernels, per_device(): pl.pallas_call(write_out, out_shape=[jax.ShapeDtypeStruct(query.shape, bf...  1.52 us

profile of v2, /device:TPU:0, one launch (start us, length us, event | category | flops | bytes accessed | tf_op | source)
XLA Modules:
  0.0 29.3 jit_solution(13522586820203951894)
XLA Ops:
  0.6 27.1 %shard_map.84 = (bf16[128,4096]{1,0:T(8,128)(2,1)S(1)}, bf16[128,4096]{1,0:T(8,128)(2,1)S(1)}, bf16[128,1024]{1,0:T(8,128)(2,1)S(1)}, bf16[128,1024]{1,0:T(8,128)(2,1)S(1)}) custom-call(s32[32]{0:T(128)} %lens_hbm.1, bf16[128,4096]{1,0:T(8,128)(2,1)} %q_hbm.1, bf16[128,1024]{1,0:T(8,128)(2,1)} %k_hbm.1, bf16[128,1024]{1,0:T(8,128)(2,1)} %v_hbm.1, ...), custom_call_target="tpu_custom_call" | custom-call | tf_op jit(solution)/shard_map/pallas_call | solution.py:272
  27.8 1.5 %shard_map.85 = (bf16[128,4096]{1,0:T(8,128)(2,1)}, bf16[128,4096]{1,0:T(8,128)(2,1)}, bf16[128,1024]{1,0:T(8,128)(2,1)}, bf16[128,1024]{1,0:T(8,128)(2,1)}) custom-call(bf16[128,4096]{1,0:T(8,128)(2,1)S(1)} %get-tuple-element.8.att, bf16[128,4096]{1,0:T(8,128)(2,1)S(1)} %get-tuple-element.9.dq, bf16[128,1024]{1,0:T(8,128)(2,1)S(1)} %get-tuple-element.10.dk, ...), custom_call_target="tpu_custom_call" | custom-call | tf_op jit(solution)/shard_map/pallas_call | solution.py:303

commit v3 on v2

--- a/solution.py
+++ b/solution.py
@@ -22,10 +22,9 @@
     rows = q_hbm.shape[0]
     kv_heads = k_hbm.shape[1] // HEAD_DIM
     groups = q_hbm.shape[1] // k_hbm.shape[1]
-    width = groups * HEAD_DIM
     span = (back + 1) * rows
     scaling = HEAD_DIM ** (-0.5)
-    chunks = kv_send.shape[1]
+    chunks = kv_recv.shape[1]
     per = kv_heads // chunks
     last = chunks - 1
     me = lax.axis_index("blk") * back + lax.axis_index("head")
@@ -46,21 +45,20 @@
         return pltpu.make_async_copy(
             (k_hbm, v_hbm)[which].at[:, columns(g, HEAD_DIM)],
             window.at[0, g, which],
-            kv_in.at[which, g],
-        )
-
-    def q_load(g, which):
-        return pltpu.make_async_copy(
-            (q_hbm, do_hbm)[which].at[:, columns(g, width)],
-            (qbuf, dobuf)[which].at[g],
-            q_in.at[which, g],
-        )
+            kv_in.at[jnp.minimum(g // per, 1)],
+        )
+
+    q_load = pltpu.make_async_copy(q_hbm, qbuf, q_in.at[0])
+    do_load = pltpu.make_async_copy(do_hbm, dobuf, q_in.at[1])
+
+    def loaded(at, which):
+        pltpu.make_async_copy(window.at[0, at], window.at[0, at], kv_in.at[which]).wait()
 
     def kv_copy(c, k):
         return pltpu.make_async_remote_copy(
             src_ref=window.at[0, heads(c)],
             dst_ref=window.at[k, heads(c)],
-            send_sem=kv_send.at[k - 1, c],
+            send_sem=kv_send.at[k - 1],
             recv_sem=kv_recv.at[k - 1, c],
             device_id=device(me + k),
             device_id_type=MESH,
@@ -80,7 +78,7 @@
         return pltpu.make_async_remote_copy(
             src_ref=part.at[k - 1, heads(c)],
             dst_ref=landed.at[k - 1, heads(c)],
-            send_sem=g_send.at[k - 1, c],
+            send_sem=g_send.at[k - 1],
             recv_sem=g_recv.at[k - 1, c],
             device_id=device(me - k),
             device_id_type=MESH,
@@ -100,32 +98,35 @@
     lens_load = pltpu.make_async_copy(lens_hbm, lens, lens_in)
     lens_load.start()
 
-    @pl.loop(0, kv_heads)
-    def _(g):
-        q_load(g, 0).start()
-        q_load(g, 1).start()
+    q_load.start()
+    do_load.start()
 
     @pl.when(me < total - 1)
     def _():
         pl.semaphore_wait(barrier, jnp.minimum(total - 1 - me, back))
 
-    def kv_loaded(c):
-        for i in range(per):
-            kv_load(c * per + i, 0).wait()
-            kv_load(c * per + i, 1).wait()
-
-    @pl.when(edge)
-    def _():
-        kv_loaded(last)
-        kv_copy(last, back).start()
-
-    @pl.loop(0, chunks - edge.astype(jnp.int32))
-    def _(c):
-        kv_loaded(c)
+    def send(c):
         for k in range(1, back + 1):
             @pl.when(me + k < total)
             def _():
                 kv_copy(c, k).start()
+
+    loaded(heads(0), 0)
+
+    @pl.when(jnp.logical_not(edge))
+    def _():
+        send(0)
+
+    loaded(pl.ds(per, kv_heads - per), 1)
+
+    @pl.when(edge)
+    def _():
+        kv_copy(last, back).start()
+        send(0)
+
+    @pl.loop(1, chunks - edge.astype(jnp.int32))
+    def _(c):
+        send(c)
 
     for k in range(1, back + 1):
         @pl.when(me - k < 0)
@@ -154,16 +155,16 @@
             a, b, (((a_dim,), (b_dim,)), ((), ())), preferred_element_type=jnp.float32
         )
 
-    def stacked(values):
+    def stacked(buf, g):
         return jnp.concatenate(
-            [values[:, h * HEAD_DIM : (h + 1) * HEAD_DIM] for h in range(groups)], axis=0
-        )
+            [buf[:, columns(g * groups + h, HEAD_DIM)] for h in range(groups)], axis=0
+        )
+
+    q_load.wait()
+    do_load.wait()
 
     @pl.loop(0, kv_heads)
     def _(g):
-        q_load(g, 0).wait()
-        q_load(g, 1).wait()
-
         @pl.when(g % per == 0)
         def _():
             for k in range(1, back + 1):
@@ -181,7 +182,7 @@
             jnp.concatenate([window[k, g, which] for k in range(back, -1, -1)], axis=0)
             for which in range(2)
         )
-        queries, grads = stacked(qbuf[g]), stacked(dobuf[g])
+        queries, grads = stacked(qbuf, g), stacked(dobuf, g)
         kept = jnp.concatenate([bias[...]] * groups, axis=1)
         scores = dot(keys, queries, 1, 1) * (scaling * math.log2(math.e)) + kept
         peak = jnp.max(scores, axis=0, keepdims=True)
@@ -233,17 +234,25 @@
     def _():
         relay().wait_send()
 
-    @pl.loop(0, chunks)
-    def _(c):
-        for k in range(1, back + 1):
-            direct = jnp.logical_not(edge & (c == last)) if k == 1 else True
-            @pl.when((me + k < total) & direct)
-            def _():
-                kv_copy(c, k).wait_send()
-
-            @pl.when(me - k >= 0)
-            def _():
-                g_copy(c, k).wait_send()
+    for k in range(1, back + 1):
+        def sent(count):
+            pltpu.make_async_copy(
+                window.at[0, pl.ds(0, count)], window.at[0, pl.ds(0, count)], kv_send.at[k - 1]
+            ).wait()
+
+        short = edge if k == 1 else jnp.bool_(False)
+
+        @pl.when((me + k < total) & jnp.logical_not(short))
+        def _():
+            sent(kv_heads)
+
+        @pl.when(short)
+        def _():
+            sent(last * per)
+
+        @pl.when(me - k >= 0)
+        def _():
+            pltpu.make_async_copy(part.at[k - 1], part.at[k - 1], g_send.at[k - 1]).wait()
 
 
 def write_out(att, dq, dk, dv, att_hbm, dq_hbm, dk_hbm, dv_hbm, sems):
@@ -264,7 +273,6 @@
 
     def per_device(query, key, value, grad_out, doc_lengths):
         rows, kv_heads = query.shape[0], key.shape[1] // HEAD_DIM
-        width = query.shape[1] // kv_heads
         chunks = kv_heads // math.gcd(kv_heads, HEADS_A_COPY)
         bf, f32 = jnp.bfloat16, jnp.float32
         anywhere = pl.BlockSpec(memory_space=pl.ANY)
@@ -281,20 +289,20 @@
             out_specs=[pl.BlockSpec(memory_space=pltpu.VMEM)] * 4,
             scratch_shapes=[
                 pltpu.VMEM((back + 1, kv_heads, 2, rows, HEAD_DIM), bf),
-                pltpu.VMEM((kv_heads, rows, width), bf),
-                pltpu.VMEM((kv_heads, rows, width), bf),
+                pltpu.VMEM(query.shape, bf),
+                pltpu.VMEM(query.shape, bf),
                 pltpu.VMEM((back, kv_heads, 2, rows, HEAD_DIM), bf),
                 pltpu.VMEM((back, kv_heads, 2, rows, HEAD_DIM), bf),
                 pltpu.VMEM((kv_heads, 2, rows, HEAD_DIM), f32),
                 pltpu.VMEM(((back + 1) * rows, rows), f32),
                 pltpu.SMEM(doc_lengths.shape, jnp.int32),
                 dma,
-                dma((2, kv_heads)),
-                dma((2, kv_heads)),
-                dma((back, chunks)),
+                dma((2,)),
+                dma((2,)),
+                dma((back,)),
                 dma((back, chunks)),
                 dma,
-                dma((back, chunks)),
+                dma((back,)),
                 dma((back, chunks)),
             ],
             compiler_params=pltpu.CompilerParams(collective_id=0, has_side_effects=True),

time: 29.5 us -> 29.2 us (0.990)
  Pallas kernels: 28.6 us -> 28.2 us
    pallas_call x1, Pallas kernels: 27.1 us -> 26.7 us  [per_device(): pl.pallas_call(functools.partial(kernel, back, total), out_shape=[pltpu.V...]
where the time goes in v3:
time: 29.2 us; the launch traced here: 28.9 us
  Pallas kernels  28.2 us (97%)
  between operations  0.64 us (2%)
    pallas_call x1, Pallas kernels, per_device(): pl.pallas_call(functools.partial(kernel, back, total), out_shape=[pltpu.V...  26.7 us
    pallas_call x1, Pallas kernels, per_device(): pl.pallas_call(write_out, out_shape=[jax.ShapeDtypeStruct(query.shape, bf...  1.52 us

profile of v3, /device:TPU:0, one launch (start us, length us, event | category | flops | bytes accessed | tf_op | source)
XLA Modules:
  0.0 28.9 jit_solution(5186450132125825196)
XLA Ops:
  0.6 26.7 %shard_map.84 = (bf16[128,4096]{1,0:T(8,128)(2,1)S(1)}, bf16[128,4096]{1,0:T(8,128)(2,1)S(1)}, bf16[128,1024]{1,0:T(8,128)(2,1)S(1)}, bf16[128,1024]{1,0:T(8,128)(2,1)S(1)}) custom-call(s32[32]{0:T(128)} %lens_hbm.1, bf16[128,4096]{1,0:T(8,128)(2,1)} %q_hbm.1, bf16[128,1024]{1,0:T(8,128)(2,1)} %k_hbm.1, bf16[128,1024]{1,0:T(8,128)(2,1)} %v_hbm.1, ...), custom_call_target="tpu_custom_call" | custom-call | tf_op jit(solution)/shard_map/pallas_call | solution.py:280
  27.4 1.5 %shard_map.85 = (bf16[128,4096]{1,0:T(8,128)(2,1)}, bf16[128,4096]{1,0:T(8,128)(2,1)}, bf16[128,1024]{1,0:T(8,128)(2,1)}, bf16[128,1024]{1,0:T(8,128)(2,1)}) custom-call(bf16[128,4096]{1,0:T(8,128)(2,1)S(1)} %get-tuple-element.8.att, bf16[128,4096]{1,0:T(8,128)(2,1)S(1)} %get-tuple-element.9.dq, bf16[128,1024]{1,0:T(8,128)(2,1)S(1)} %get-tuple-element.10.dk, ...), custom_call_target="tpu_custom_call" | custom-call | tf_op jit(solution)/shard_map/pallas_call | solution.py:311

commit v4 on v3

--- a/solution.py
+++ b/solution.py
@@ -16,8 +16,8 @@
 
 def kernel(
     back, total, lens_hbm, q_hbm, k_hbm, v_hbm, do_hbm, attbuf, dqbuf, dkbuf, dvbuf,
-    window, qbuf, dobuf, part, landed, own, bias, lens,
-    lens_in, kv_in, q_in, kv_send, kv_recv, relay_send, g_send, g_recv,
+    window, qbuf, dobuf, part, landed, passing, own, bias, lens,
+    lens_in, kv_in, q_in, kv_send, kv_recv, relay_send, g_send, g_recv, pass_recv, pass_send,
 ):
     rows = q_hbm.shape[0]
     kv_heads = k_hbm.shape[1] // HEAD_DIM
@@ -31,6 +31,8 @@
     place = me % (2 * back)
     edge = (place == 2 * back - 1) & (me + back < total) & (back == 2)
     relays = (place == 1) & (me > back) & (back == 2)
+    around = (place == 0) & (me > back) & (back == 2)
+    passes = (place == 2) & (me + back < total) & (back == 2)
 
     def device(number):
         return {"blk": number // back, "head": number % back}
@@ -64,6 +66,16 @@
             device_id_type=MESH,
         )
 
+    def first_copy(g, which, k):
+        return pltpu.make_async_remote_copy(
+            src_ref=(k_hbm, v_hbm)[which].at[:, columns(g, HEAD_DIM)],
+            dst_ref=window.at[k, g, which],
+            send_sem=kv_send.at[k - 1],
+            recv_sem=kv_recv.at[k - 1, 0],
+            device_id=device(me + k),
+            device_id_type=MESH,
+        )
+
     def relay():
         return pltpu.make_async_remote_copy(
             src_ref=window.at[back, heads(last)],
@@ -74,21 +86,42 @@
             device_id_type=MESH,
         )
 
-    def g_copy(c, k):
+    def g_copy(g, k):
         return pltpu.make_async_remote_copy(
-            src_ref=part.at[k - 1, heads(c)],
-            dst_ref=landed.at[k - 1, heads(c)],
+            src_ref=part.at[k - 1, g],
+            dst_ref=landed.at[k - 1, g],
             send_sem=g_send.at[k - 1],
-            recv_sem=g_recv.at[k - 1, c],
+            recv_sem=g_recv.at[k - 1, g // per],
             device_id=device(me - k),
             device_id_type=MESH,
         )
+
+    def g_landed(c, k):
+        at = landed.at[k - 1, heads(c)]
+        pltpu.make_async_copy(at, at, g_recv.at[k - 1, c]).wait()
 
     barrier = pltpu.get_barrier_semaphore()
     for k in range(1, back + 1):
         @pl.when(me - k >= 0)
         def _():
             pl.semaphore_signal(barrier, inc=1, device_id=device(me - k), device_id_type=MESH)
+
+    around_copy = pltpu.make_async_remote_copy(
+        src_ref=part.at[0, heads(0)],
+        dst_ref=passing,
+        send_sem=g_send.at[0],
+        recv_sem=pass_recv,
+        device_id=device(me - back),
+        device_id_type=MESH,
+    )
+    pass_copy = pltpu.make_async_remote_copy(
+        src_ref=passing,
+        dst_ref=landed.at[0, heads(0)],
+        send_sem=pass_send,
+        recv_sem=g_recv.at[0, 0],
+        device_id=device(me + 1),
+        device_id_type=MESH,
+    )
 
     @pl.loop(0, kv_heads)
     def _(g):
@@ -98,35 +131,38 @@
     lens_load = pltpu.make_async_copy(lens_hbm, lens, lens_in)
     lens_load.start()
 
-    q_load.start()
-    do_load.start()
 
     @pl.when(me < total - 1)
     def _():
         pl.semaphore_wait(barrier, jnp.minimum(total - 1 - me, back))
 
-    def send(c):
-        for k in range(1, back + 1):
-            @pl.when(me + k < total)
-            def _():
-                kv_copy(c, k).start()
-
+    def first(k):
+        for g in range(per):
+            for which in range(2):
+                first_copy(g, which, k).start()
+
+    for k in range(1, back + 1):
+        @pl.when((me + k < total) & jnp.logical_not(edge if k == back else False))
+        def _():
+            first(k)
+
+    q_load.start()
+    do_load.start()
     loaded(heads(0), 0)
-
-    @pl.when(jnp.logical_not(edge))
-    def _():
-        send(0)
-
     loaded(pl.ds(per, kv_heads - per), 1)
 
     @pl.when(edge)
     def _():
         kv_copy(last, back).start()
-        send(0)
+        first(back)
 
     @pl.loop(1, chunks - edge.astype(jnp.int32))
     def _(c):
-        send(c)
+        for k in range(1, back + 1):
+            later = relays & (c == last) if k == 1 else False
+            @pl.when((me + k < total) & jnp.logical_not(later))
+            def _():
+                kv_copy(c, k).start()
 
     for k in range(1, back + 1):
         @pl.when(me - k < 0)
@@ -177,6 +213,12 @@
         def _():
             kv_copy(last, back).wait_recv()
             relay().start()
+            kv_copy(last, 1).start()
+
+        @pl.when(passes & (g == kv_heads - 1))
+        def _():
+            around_copy.wait_recv()
+            pass_copy.start()
 
         keys, values = (
             jnp.concatenate([window[k, g, which] for k in range(back, -1, -1)], axis=0)
@@ -203,12 +245,15 @@
         own[g, 0] = grad_key[back * rows :]
         own[g, 1] = grad_value[back * rows :]
 
-        @pl.when(g % per == per - 1)
-        def _():
-            for k in range(1, back + 1):
-                @pl.when(me - k >= 0)
-                def _():
-                    g_copy(g // per, k).start()
+        @pl.when(around & (g == per - 1))
+        def _():
+            around_copy.start()
+
+        for k in range(back, 0, -1):
+            detour = around & (g < per) if k == 1 else False
+            @pl.when((me - k >= 0) & jnp.logical_not(detour))
+            def _():
+                g_copy(g, k).start()
 
         for h in range(groups):
             at = slice(h * HEAD_DIM, (h + 1) * HEAD_DIM)
@@ -221,7 +266,7 @@
         for k in range(1, back + 1):
             @pl.when(me + k < total)
             def _():
-                g_copy(c, k).wait_recv()
+                g_landed(c, k)
         for i in range(per):
             g = c * per + i
             sums = own[g]
@@ -233,6 +278,10 @@
     @pl.when(relays)
     def _():
         relay().wait_send()
+
+    @pl.when(passes)
+    def _():
+        pass_copy.wait_send()
 
     for k in range(1, back + 1):
         def sent(count):
@@ -293,6 +342,7 @@
                 pltpu.VMEM(query.shape, bf),
                 pltpu.VMEM((back, kv_heads, 2, rows, HEAD_DIM), bf),
                 pltpu.VMEM((back, kv_heads, 2, rows, HEAD_DIM), bf),
+                pltpu.VMEM((kv_heads // chunks, 2, rows, HEAD_DIM), bf),
                 pltpu.VMEM((kv_heads, 2, rows, HEAD_DIM), f32),
                 pltpu.VMEM(((back + 1) * rows, rows), f32),
                 pltpu.SMEM(doc_lengths.shape, jnp.int32),
@@ -304,6 +354,8 @@
                 dma,
                 dma((back,)),
                 dma((back, chunks)),
+                dma,
+                dma,
             ],
             compiler_params=pltpu.CompilerParams(collective_id=0, has_side_effects=True),
         )(doc_lengths, query, key, value, grad_out)

time: 29.2 us -> 28.6 us (0.979)
  Pallas kernels: 28.2 us -> 27.8 us
    pallas_call x1, Pallas kernels: 26.7 us -> 26.3 us  [per_device(): pl.pallas_call(functools.partial(kernel, back, total), out_shape=[pltpu.V...]
where the time goes in v4:
time: 28.6 us; the launch traced here: 28.5 us
  Pallas kernels  27.8 us (97%)
  between operations  0.64 us (2%)
    pallas_call x1, Pallas kernels, per_device(): pl.pallas_call(functools.partial(kernel, back, total), out_shape=[pltpu.V...  26.3 us
    pallas_call x1, Pallas kernels, per_device(): pl.pallas_call(write_out, out_shape=[jax.ShapeDtypeStruct(query.shape, bf...  1.52 us

profile of v4, /device:TPU:0, one launch (start us, length us, event | category | flops | bytes accessed | tf_op | source)
XLA Modules:
  0.0 28.5 jit_solution(15418916940253606772)
XLA Ops:
  0.6 26.3 %shard_map.84 = (bf16[128,4096]{1,0:T(8,128)(2,1)S(1)}, bf16[128,4096]{1,0:T(8,128)(2,1)S(1)}, bf16[128,1024]{1,0:T(8,128)(2,1)S(1)}, bf16[128,1024]{1,0:T(8,128)(2,1)S(1)}) custom-call(s32[32]{0:T(128)} %lens_hbm.1, bf16[128,4096]{1,0:T(8,128)(2,1)} %q_hbm.1, bf16[128,1024]{1,0:T(8,128)(2,1)} %k_hbm.1, bf16[128,1024]{1,0:T(8,128)(2,1)} %v_hbm.1, ...), custom_call_target="tpu_custom_call" | custom-call | tf_op jit(solution)/shard_map/pallas_call | solution.py:329
  26.9 1.5 %shard_map.85 = (bf16[128,4096]{1,0:T(8,128)(2,1)}, bf16[128,4096]{1,0:T(8,128)(2,1)}, bf16[128,1024]{1,0:T(8,128)(2,1)}, bf16[128,1024]{1,0:T(8,128)(2,1)}) custom-call(bf16[128,4096]{1,0:T(8,128)(2,1)S(1)} %get-tuple-element.8.att, bf16[128,4096]{1,0:T(8,128)(2,1)S(1)} %get-tuple-element.9.dq, bf16[128,1024]{1,0:T(8,128)(2,1)S(1)} %get-tuple-element.10.dk, ...), custom_call_target="tpu_custom_call" | custom-call | tf_op jit(solution)/shard_map/pallas_call | solution.py:363

commit v5 on v4

--- a/solution.py
+++ b/solution.py
@@ -16,15 +16,15 @@
 
 def kernel(
     back, total, lens_hbm, q_hbm, k_hbm, v_hbm, do_hbm, attbuf, dqbuf, dkbuf, dvbuf,
-    window, qbuf, dobuf, part, landed, passing, own, bias, lens,
-    lens_in, kv_in, q_in, kv_send, kv_recv, relay_send, g_send, g_recv, pass_recv, pass_send,
+    window, qbuf, part, landed, passing, own, bias, lens,
+    lens_in, kv_in, q_in, kv_send, kv_recv, edge_recv, relay_send, g_send, g_recv, pass_recv, pass_send,
 ):
     rows = q_hbm.shape[0]
     kv_heads = k_hbm.shape[1] // HEAD_DIM
     groups = q_hbm.shape[1] // k_hbm.shape[1]
     span = (back + 1) * rows
     scaling = HEAD_DIM ** (-0.5)
-    chunks = kv_recv.shape[1]
+    chunks = g_recv.shape[0]
     per = kv_heads // chunks
     last = chunks - 1
     me = lax.axis_index("blk") * back + lax.axis_index("head")
@@ -47,21 +47,21 @@
         return pltpu.make_async_copy(
             (k_hbm, v_hbm)[which].at[:, columns(g, HEAD_DIM)],
             window.at[0, g, which],
-            kv_in.at[jnp.minimum(g // per, 1)],
-        )
-
-    q_load = pltpu.make_async_copy(q_hbm, qbuf, q_in.at[0])
-    do_load = pltpu.make_async_copy(do_hbm, dobuf, q_in.at[1])
-
-    def loaded(at, which):
-        pltpu.make_async_copy(window.at[0, at], window.at[0, at], kv_in.at[which]).wait()
+            kv_in,
+        )
+
+    q_load = pltpu.make_async_copy(q_hbm, qbuf.at[0], q_in)
+    do_load = pltpu.make_async_copy(do_hbm, qbuf.at[1], q_in)
+
+    def wait_for(landing, sem):
+        pltpu.make_async_copy(landing, landing, sem).wait()
 
     def kv_copy(c, k):
         return pltpu.make_async_remote_copy(
             src_ref=window.at[0, heads(c)],
             dst_ref=window.at[k, heads(c)],
             send_sem=kv_send.at[k - 1],
-            recv_sem=kv_recv.at[k - 1, c],
+            recv_sem=kv_recv.at[c],
             device_id=device(me + k),
             device_id_type=MESH,
         )
@@ -71,17 +71,26 @@
             src_ref=(k_hbm, v_hbm)[which].at[:, columns(g, HEAD_DIM)],
             dst_ref=window.at[k, g, which],
             send_sem=kv_send.at[k - 1],
-            recv_sem=kv_recv.at[k - 1, 0],
+            recv_sem=kv_recv.at[0],
             device_id=device(me + k),
             device_id_type=MESH,
         )
+
+    edge_copy = pltpu.make_async_remote_copy(
+        src_ref=window.at[0, heads(last)],
+        dst_ref=window.at[back, heads(last)],
+        send_sem=kv_send.at[back - 1],
+        recv_sem=edge_recv,
+        device_id=device(me + back),
+        device_id_type=MESH,
+    )
 
     def relay():
         return pltpu.make_async_remote_copy(
             src_ref=window.at[back, heads(last)],
             dst_ref=window.at[1, heads(last)],
             send_sem=relay_send,
-            recv_sem=kv_recv.at[0, last],
+            recv_sem=kv_recv.at[last],
             device_id=device(me - 1),
             device_id_type=MESH,
         )
@@ -91,14 +100,10 @@
             src_ref=part.at[k - 1, g],
             dst_ref=landed.at[k - 1, g],
             send_sem=g_send.at[k - 1],
-            recv_sem=g_recv.at[k - 1, g // per],
+            recv_sem=g_recv.at[g // per],
             device_id=device(me - k),
             device_id_type=MESH,
         )
-
-    def g_landed(c, k):
-        at = landed.at[k - 1, heads(c)]
-        pltpu.make_async_copy(at, at, g_recv.at[k - 1, c]).wait()
 
     barrier = pltpu.get_barrier_semaphore()
     for k in range(1, back + 1):
@@ -118,15 +123,17 @@
         src_ref=passing,
         dst_ref=landed.at[0, heads(0)],
         send_sem=pass_send,
-        recv_sem=g_recv.at[0, 0],
+        recv_sem=g_recv.at[0],
         device_id=device(me + 1),
         device_id_type=MESH,
     )
 
-    @pl.loop(0, kv_heads)
-    def _(g):
-        kv_load(g, 0).start()
-        kv_load(g, 1).start()
+    @pl.when(place != 1)
+    def _():
+        @pl.loop(0, kv_heads)
+        def _(g):
+            kv_load(g, 0).start()
+            kv_load(g, 1).start()
 
     lens_load = pltpu.make_async_copy(lens_hbm, lens, lens_in)
     lens_load.start()
@@ -146,14 +153,18 @@
         def _():
             first(k)
 
-    q_load.start()
-    do_load.start()
-    loaded(heads(0), 0)
-    loaded(pl.ds(per, kv_heads - per), 1)
+    @pl.when(place == 1)
+    def _():
+        @pl.loop(0, kv_heads)
+        def _(g):
+            kv_load(g, 0).start()
+            kv_load(g, 1).start()
+
+    wait_for(window.at[0], kv_in)
 
     @pl.when(edge)
     def _():
-        kv_copy(last, back).start()
+        edge_copy.start()
         first(back)
 
     @pl.loop(1, chunks - edge.astype(jnp.int32))
@@ -164,6 +175,9 @@
             def _():
                 kv_copy(c, k).start()
 
+    q_load.start()
+    do_load.start()
+
     for k in range(1, back + 1):
         @pl.when(me - k < 0)
         def _():
@@ -191,27 +205,26 @@
             a, b, (((a_dim,), (b_dim,)), ((), ())), preferred_element_type=jnp.float32
         )
 
-    def stacked(buf, g):
+    def stacked(which, g):
         return jnp.concatenate(
-            [buf[:, columns(g * groups + h, HEAD_DIM)] for h in range(groups)], axis=0
-        )
-
-    q_load.wait()
-    do_load.wait()
+            [qbuf[which, :, columns(g * groups + h, HEAD_DIM)] for h in range(groups)], axis=0
+        )
+
+    wait_for(qbuf, q_in)
 
     @pl.loop(0, kv_heads)
     def _(g):
         @pl.when(g % per == 0)
         def _():
-            for k in range(1, back + 1):
-                early = relays & (g // per == last) if k == back else False
-                @pl.when((me - k >= 0) & jnp.logical_not(early))
+            early = relays & (g == last * per)
+            for n in range(1, back + 1):
+                @pl.when((jnp.minimum(me, back) - early.astype(jnp.int32)) == n)
                 def _():
-                    kv_copy(g // per, k).wait_recv()
+                    wait_for(window.at[pl.ds(1, n), heads(g // per)], kv_recv.at[g // per])
 
         @pl.when(relays & (g == 0))
         def _():
-            kv_copy(last, back).wait_recv()
+            edge_copy.wait_recv()
             relay().start()
             kv_copy(last, 1).start()
 
@@ -224,7 +237,7 @@
             jnp.concatenate([window[k, g, which] for k in range(back, -1, -1)], axis=0)
             for which in range(2)
         )
-        queries, grads = stacked(qbuf, g), stacked(dobuf, g)
+        queries, grads = stacked(0, g), stacked(1, g)
         kept = jnp.concatenate([bias[...]] * groups, axis=1)
         scores = dot(keys, queries, 1, 1) * (scaling * math.log2(math.e)) + kept
         peak = jnp.max(scores, axis=0, keepdims=True)
@@ -263,10 +276,11 @@
 
     @pl.loop(0, chunks)
     def _(c):
-        for k in range(1, back + 1):
-            @pl.when(me + k < total)
+        for n in range(1, back + 1):
+            @pl.when(jnp.minimum(total - 1 - me, back) == n)
             def _():
-                g_landed(c, k)
+                wait_for(landed.at[pl.ds(0, n), heads(c)], g_recv.at[c])
+
         for i in range(per):
             g = c * per + i
             sums = own[g]
@@ -284,24 +298,19 @@
         pass_copy.wait_send()
 
     for k in range(1, back + 1):
-        def sent(count):
-            pltpu.make_async_copy(
-                window.at[0, pl.ds(0, count)], window.at[0, pl.ds(0, count)], kv_send.at[k - 1]
-            ).wait()
-
         short = edge if k == 1 else jnp.bool_(False)
 
         @pl.when((me + k < total) & jnp.logical_not(short))
         def _():
-            sent(kv_heads)
+            wait_for(window.at[0], kv_send.at[k - 1])
 
         @pl.when(short)
         def _():
-            sent(last * per)
+            wait_for(window.at[0, pl.ds(0, last * per)], kv_send.at[k - 1])
 
         @pl.when(me - k >= 0)
         def _():
-            pltpu.make_async_copy(part.at[k - 1], part.at[k - 1], g_send.at[k - 1]).wait()
+            wait_for(part.at[k - 1], g_send.at[k - 1])
 
 
 def write_out(att, dq, dk, dv, att_hbm, dq_hbm, dk_hbm, dv_hbm, sems):
@@ -338,8 +347,7 @@
             out_specs=[pl.BlockSpec(memory_space=pltpu.VMEM)] * 4,
             scratch_shapes=[
                 pltpu.VMEM((back + 1, kv_heads, 2, rows, HEAD_DIM), bf),
-                pltpu.VMEM(query.shape, bf),
-                pltpu.VMEM(query.shape, bf),
+                pltpu.VMEM((2, *query.shape), bf),
                 pltpu.VMEM((back, kv_heads, 2, rows, HEAD_DIM), bf),
                 pltpu.VMEM((back, kv_heads, 2, rows, HEAD_DIM), bf),
                 pltpu.VMEM((kv_heads // chunks, 2, rows, HEAD_DIM), bf),
@@ -347,13 +355,14 @@
                 pltpu.VMEM(((back + 1) * rows, rows), f32),
                 pltpu.SMEM(doc_lengths.shape, jnp.int32),
                 dma,
-                dma((2,)),
-                dma((2,)),
+                dma,
+                dma,
                 dma((back,)),
-                dma((back, chunks)),
+                dma((chunks,)),
+                dma,
                 dma,
                 dma((back,)),
-                dma((back, chunks)),
+                dma((chunks,)),
                 dma,
                 dma,
             ],

time: 28.6 us -> 28.5 us (level)
  no operation moved by 1% of the time
where the time goes in v5:
time: 28.5 us; the launch traced here: 28.3 us
  Pallas kernels  27.6 us (97%)
  between operations  0.64 us (2%)
    pallas_call x1, Pallas kernels, per_device(): pl.pallas_call(functools.partial(kernel, back, total), out_shape=[pltpu.V...  26.1 us
    pallas_call x1, Pallas kernels, per_device(): pl.pallas_call(write_out, out_shape=[jax.ShapeDtypeStruct(query.shape, bf...  1.52 us

profile of v5, /device:TPU:0, one launch (start us, length us, event | category | flops | bytes accessed | tf_op | source)
XLA Modules:
  0.0 28.3 jit_solution(5339271478144915058)
XLA Ops:
  0.6 26.1 %shard_map.84 = (bf16[128,4096]{1,0:T(8,128)(2,1)S(1)}, bf16[128,4096]{1,0:T(8,128)(2,1)S(1)}, bf16[128,1024]{1,0:T(8,128)(2,1)S(1)}, bf16[128,1024]{1,0:T(8,128)(2,1)S(1)}) custom-call(s32[32]{0:T(128)} %lens_hbm.1, bf16[128,4096]{1,0:T(8,128)(2,1)} %q_hbm.1, bf16[128,1024]{1,0:T(8,128)(2,1)} %k_hbm.1, bf16[128,1024]{1,0:T(8,128)(2,1)} %v_hbm.1, ...), custom_call_target="tpu_custom_call" | custom-call | tf_op jit(solution)/shard_map/pallas_call | solution.py:338
  26.7 1.5 %shard_map.85 = (bf16[128,4096]{1,0:T(8,128)(2,1)}, bf16[128,4096]{1,0:T(8,128)(2,1)}, bf16[128,1024]{1,0:T(8,128)(2,1)}, bf16[128,1024]{1,0:T(8,128)(2,1)}) custom-call(bf16[128,4096]{1,0:T(8,128)(2,1)S(1)} %get-tuple-element.8.att, bf16[128,4096]{1,0:T(8,128)(2,1)S(1)} %get-tuple-element.9.dq, bf16[128,1024]{1,0:T(8,128)(2,1)S(1)} %get-tuple-element.10.dk, ...), custom_call_target="tpu_custom_call" | custom-call | tf_op jit(solution)/shard_map/pallas_call | solution.py:372

commit v6 on v5

--- a/solution.py
+++ b/solution.py
@@ -128,49 +128,44 @@
         device_id_type=MESH,
     )
 
-    @pl.when(place != 1)
-    def _():
+    eager = place == 1
+
+    def load():
         @pl.loop(0, kv_heads)
         def _(g):
             kv_load(g, 0).start()
             kv_load(g, 1).start()
 
+    @pl.when(jnp.logical_not(eager))
+    def _():
+        load()
+
+    @pl.when(me < total - 1)
+    def _():
+        pl.semaphore_wait(barrier, jnp.minimum(total - 1 - me, back))
+
+    @pl.when(eager)
+    def _():
+        for g in range(per):
+            for which in range(2):
+                first_copy(g, which, 1).start()
+
+        load()
+
     lens_load = pltpu.make_async_copy(lens_hbm, lens, lens_in)
     lens_load.start()
-
-
-    @pl.when(me < total - 1)
-    def _():
-        pl.semaphore_wait(barrier, jnp.minimum(total - 1 - me, back))
-
-    def first(k):
-        for g in range(per):
-            for which in range(2):
-                first_copy(g, which, k).start()
-
-    for k in range(1, back + 1):
-        @pl.when((me + k < total) & jnp.logical_not(edge if k == back else False))
-        def _():
-            first(k)
-
-    @pl.when(place == 1)
-    def _():
-        @pl.loop(0, kv_heads)
-        def _(g):
-            kv_load(g, 0).start()
-            kv_load(g, 1).start()
-
     wait_for(window.at[0], kv_in)
 
     @pl.when(edge)
     def _():
+        kv_copy(0, 1).start()
         edge_copy.start()
-        first(back)
-
-    @pl.loop(1, chunks - edge.astype(jnp.int32))
+        kv_copy(0, back).start()
+
+    @pl.loop(edge.astype(jnp.int32), chunks - edge.astype(jnp.int32))
     def _(c):
         for k in range(1, back + 1):
-            later = relays & (c == last) if k == 1 else False
+            later = (relays & (c == last)) | (eager & (c == 0)) if k == 1 else False
             @pl.when((me + k < total) & jnp.logical_not(later))
             def _():
                 kv_copy(c, k).start()

time: 28.5 us -> 28.5 us (level)
  no operation moved by 1% of the time
where the time goes in v6:
time: 28.5 us; the launch traced here: 28.3 us
  Pallas kernels  27.6 us (97%)
  between operations  0.64 us (2%)
    pallas_call x1, Pallas kernels, per_device(): pl.pallas_call(functools.partial(kernel, back, total), out_shape=[pltpu.V...  26.1 us
    pallas_call x1, Pallas kernels, per_device(): pl.pallas_call(write_out, out_shape=[jax.ShapeDtypeStruct(query.shape, bf...  1.52 us

profile of v6, /device:TPU:0, one launch (start us, length us, event | category | flops | bytes accessed | tf_op | source)
XLA Modules:
  0.0 28.3 jit_solution(1620263887512126732)
XLA Ops:
  0.6 26.1 %shard_map.84 = (bf16[128,4096]{1,0:T(8,128)(2,1)S(1)}, bf16[128,4096]{1,0:T(8,128)(2,1)S(1)}, bf16[128,1024]{1,0:T(8,128)(2,1)S(1)}, bf16[128,1024]{1,0:T(8,128)(2,1)S(1)}) custom-call(s32[32]{0:T(128)} %lens_hbm.1, bf16[128,4096]{1,0:T(8,128)(2,1)} %q_hbm.1, bf16[128,1024]{1,0:T(8,128)(2,1)} %k_hbm.1, bf16[128,1024]{1,0:T(8,128)(2,1)} %v_hbm.1, ...), custom_call_target="tpu_custom_call" | custom-call | tf_op jit(solution)/shard_map/pallas_call | solution.py:333
  26.7 1.5 %shard_map.85 = (bf16[128,4096]{1,0:T(8,128)(2,1)}, bf16[128,4096]{1,0:T(8,128)(2,1)}, bf16[128,1024]{1,0:T(8,128)(2,1)}, bf16[128,1024]{1,0:T(8,128)(2,1)}) custom-call(bf16[128,4096]{1,0:T(8,128)(2,1)S(1)} %get-tuple-element.8.att, bf16[128,4096]{1,0:T(8,128)(2,1)S(1)} %get-tuple-element.9.dq, bf16[128,1024]{1,0:T(8,128)(2,1)S(1)} %get-tuple-element.10.dk, ...), custom_call_target="tpu_custom_call" | custom-call | tf_op jit(solution)/shard_map/pallas_call | solution.py:367

commit v7 on v6

--- a/solution.py
+++ b/solution.py
@@ -17,7 +17,7 @@
 def kernel(
     back, total, lens_hbm, q_hbm, k_hbm, v_hbm, do_hbm, attbuf, dqbuf, dkbuf, dvbuf,
     window, qbuf, part, landed, passing, own, bias, lens,
-    lens_in, kv_in, q_in, kv_send, kv_recv, edge_recv, relay_send, g_send, g_recv, pass_recv, pass_send,
+    lens_in, kv_in, kv_send, kv_recv, detour_recv, detour_send, g_send, g_recv,
 ):
     rows = q_hbm.shape[0]
     kv_heads = k_hbm.shape[1] // HEAD_DIM
@@ -50,8 +50,8 @@
             kv_in,
         )
 
-    q_load = pltpu.make_async_copy(q_hbm, qbuf.at[0], q_in)
-    do_load = pltpu.make_async_copy(do_hbm, qbuf.at[1], q_in)
+    q_load = pltpu.make_async_copy(q_hbm, qbuf.at[0], kv_in)
+    do_load = pltpu.make_async_copy(do_hbm, qbuf.at[1], kv_in)
 
     def wait_for(landing, sem):
         pltpu.make_async_copy(landing, landing, sem).wait()
@@ -80,7 +80,7 @@
         src_ref=window.at[0, heads(last)],
         dst_ref=window.at[back, heads(last)],
         send_sem=kv_send.at[back - 1],
-        recv_sem=edge_recv,
+        recv_sem=detour_recv,
         device_id=device(me + back),
         device_id_type=MESH,
     )
@@ -89,7 +89,7 @@
         return pltpu.make_async_remote_copy(
             src_ref=window.at[back, heads(last)],
             dst_ref=window.at[1, heads(last)],
-            send_sem=relay_send,
+            send_sem=detour_send,
             recv_sem=kv_recv.at[last],
             device_id=device(me - 1),
             device_id_type=MESH,
@@ -115,14 +115,14 @@
         src_ref=part.at[0, heads(0)],
         dst_ref=passing,
         send_sem=g_send.at[0],
-        recv_sem=pass_recv,
+        recv_sem=detour_recv,
         device_id=device(me - back),
         device_id_type=MESH,
     )
     pass_copy = pltpu.make_async_remote_copy(
         src_ref=passing,
         dst_ref=landed.at[0, heads(0)],
-        send_sem=pass_send,
+        send_sem=detour_send,
         recv_sem=g_recv.at[0],
         device_id=device(me + 1),
         device_id_type=MESH,
@@ -205,7 +205,7 @@
             [qbuf[which, :, columns(g * groups + h, HEAD_DIM)] for h in range(groups)], axis=0
         )
 
-    wait_for(qbuf, q_in)
+    wait_for(qbuf, kv_in)
 
     @pl.loop(0, kv_heads)
     def _(g):
@@ -269,8 +269,7 @@
             attbuf[:, to] = attended[:, at].T.astype(jnp.bfloat16)
             dqbuf[:, to] = grad_query[:, at].T.astype(jnp.bfloat16)
 
-    @pl.loop(0, chunks)
-    def _(c):
+    def total_up(c):
         for n in range(1, back + 1):
             @pl.when(jnp.minimum(total - 1 - me, back) == n)
             def _():
@@ -284,6 +283,10 @@
             dkbuf[:, columns(g, HEAD_DIM)] = sums[0].astype(jnp.bfloat16)
             dvbuf[:, columns(g, HEAD_DIM)] = sums[1].astype(jnp.bfloat16)
 
+    @pl.loop(0, last)
+    def _(c):
+        total_up(c)
+
     @pl.when(relays)
     def _():
         relay().wait_send()
@@ -306,6 +309,8 @@
         @pl.when(me - k >= 0)
         def _():
             wait_for(part.at[k - 1], g_send.at[k - 1])
+
+    total_up(last)
 
 
 def write_out(att, dq, dk, dv, att_hbm, dq_hbm, dk_hbm, dv_hbm, sems):
@@ -351,15 +356,12 @@
                 pltpu.SMEM(doc_lengths.shape, jnp.int32),
                 dma,
                 dma,
-                dma,
                 dma((back,)),
                 dma((chunks,)),
                 dma,
                 dma,
                 dma((back,)),
                 dma((chunks,)),
-                dma,
-                dma,
             ],
             compiler_params=pltpu.CompilerParams(collective_id=0, has_side_effects=True),
         )(doc_lengths, query, key, value, grad_out)

time: 28.5 us -> 28.4 us (level)
  no operation moved by 1% of the time
where the time goes in v7:
time: 28.4 us; the launch traced here: 28.2 us
  Pallas kernels  27.6 us (97%)
  between operations  0.64 us (2%)
    pallas_call x1, Pallas kernels, per_device(): pl.pallas_call(functools.partial(kernel, back, total), out_shape=[pltpu.V...  26.1 us
    pallas_call x1, Pallas kernels, per_device(): pl.pallas_call(write_out, out_shape=[jax.ShapeDtypeStruct(query.shape, bf...  1.52 us

profile of v7, /device:TPU:0, one launch (start us, length us, event | category | flops | bytes accessed | tf_op | source)
XLA Modules:
  0.0 28.2 jit_solution(13408301257524103218)
XLA Ops:
  0.6 26.1 %shard_map.84 = (bf16[128,4096]{1,0:T(8,128)(2,1)S(1)}, bf16[128,4096]{1,0:T(8,128)(2,1)S(1)}, bf16[128,1024]{1,0:T(8,128)(2,1)S(1)}, bf16[128,1024]{1,0:T(8,128)(2,1)S(1)}) custom-call(s32[32]{0:T(128)} %lens_hbm.1, bf16[128,4096]{1,0:T(8,128)(2,1)} %q_hbm.1, bf16[128,1024]{1,0:T(8,128)(2,1)} %k_hbm.1, bf16[128,1024]{1,0:T(8,128)(2,1)} %v_hbm.1, ...), custom_call_target="tpu_custom_call" | custom-call | tf_op jit(solution)/shard_map/pallas_call | solution.py:338
  26.7 1.5 %shard_map.85 = (bf16[128,4096]{1,0:T(8,128)(2,1)}, bf16[128,4096]{1,0:T(8,128)(2,1)}, bf16[128,1024]{1,0:T(8,128)(2,1)}, bf16[128,1024]{1,0:T(8,128)(2,1)}) custom-call(bf16[128,4096]{1,0:T(8,128)(2,1)S(1)} %get-tuple-element.8.att, bf16[128,4096]{1,0:T(8,128)(2,1)S(1)} %get-tuple-element.9.dq, bf16[128,1024]{1,0:T(8,128)(2,1)S(1)} %get-tuple-element.10.dk, ...), custom_call_target="tpu_custom_call" | custom-call | tf_op jit(solution)/shard_map/pallas_call | solution.py:369

commit v8 on v7

--- a/solution.py
+++ b/solution.py
@@ -223,7 +223,7 @@
             relay().start()
             kv_copy(last, 1).start()
 
-        @pl.when(passes & (g == kv_heads - 1))
+        @pl.when(passes & (g == kv_heads - 2))
         def _():
             around_copy.wait_recv()
             pass_copy.start()

time: 28.4 us -> 28.4 us (level)
  no operation moved by 1% of the time
where the time goes in v8:
time: 28.4 us; the launch traced here: 28.2 us
  Pallas kernels  27.6 us (97%)
  between operations  0.64 us (2%)
    pallas_call x1, Pallas kernels, per_device(): pl.pallas_call(functools.partial(kernel, back, total), out_shape=[pltpu.V...  26.1 us
    pallas_call x1, Pallas kernels, per_device(): pl.pallas_call(write_out, out_shape=[jax.ShapeDtypeStruct(query.shape, bf...  1.52 us

profile of v8, /device:TPU:0, one launch (start us, length us, event | category | flops | bytes accessed | tf_op | source)
XLA Modules:
  0.0 28.2 jit_solution(2607189589472804532)
XLA Ops:
  0.6 26.1 %shard_map.84 = (bf16[128,4096]{1,0:T(8,128)(2,1)S(1)}, bf16[128,4096]{1,0:T(8,128)(2,1)S(1)}, bf16[128,1024]{1,0:T(8,128)(2,1)S(1)}, bf16[128,1024]{1,0:T(8,128)(2,1)S(1)}) custom-call(s32[32]{0:T(128)} %lens_hbm.1, bf16[128,4096]{1,0:T(8,128)(2,1)} %q_hbm.1, bf16[128,1024]{1,0:T(8,128)(2,1)} %k_hbm.1, bf16[128,1024]{1,0:T(8,128)(2,1)} %v_hbm.1, ...), custom_call_target="tpu_custom_call" | custom-call | tf_op jit(solution)/shard_map/pallas_call | solution.py:338
  26.7 1.5 %shard_map.85 = (bf16[128,4096]{1,0:T(8,128)(2,1)}, bf16[128,4096]{1,0:T(8,128)(2,1)}, bf16[128,1024]{1,0:T(8,128)(2,1)}, bf16[128,1024]{1,0:T(8,128)(2,1)}) custom-call(bf16[128,4096]{1,0:T(8,128)(2,1)S(1)} %get-tuple-element.8.att, bf16[128,4096]{1,0:T(8,128)(2,1)S(1)} %get-tuple-element.9.dq, bf16[128,1024]{1,0:T(8,128)(2,1)S(1)} %get-tuple-element.10.dk, ...), custom_call_target="tpu_custom_call" | custom-call | tf_op jit(solution)/shard_map/pallas_call | solution.py:369

commit v9 on v7

--- a/solution.py
+++ b/solution.py
@@ -170,18 +170,18 @@
             def _():
                 kv_copy(c, k).start()
 
+
+    for k in range(1, back + 1):
+        @pl.when(me - k < 0)
+        def _():
+            window[k] = jnp.zeros((kv_heads, 2, rows, HEAD_DIM), jnp.bfloat16)
+
+        @pl.when(me + k >= total)
+        def _():
+            landed[k - 1] = jnp.zeros((kv_heads, 2, rows, HEAD_DIM), jnp.bfloat16)
+
     q_load.start()
     do_load.start()
-
-    for k in range(1, back + 1):
-        @pl.when(me - k < 0)
-        def _():
-            window[k] = jnp.zeros((kv_heads, 2, rows, HEAD_DIM), jnp.bfloat16)
-
-        @pl.when(me + k >= total)
-        def _():
-            landed[k - 1] = jnp.zeros((kv_heads, 2, rows, HEAD_DIM), jnp.bfloat16)
-
     lens_load.wait()
     query_pos = me * rows + lax.broadcasted_iota(jnp.int32, (1, rows), 1)
 

time: 28.4 us -> 28.4 us (level)
  no operation moved by 1% of the time
where the time goes in v9:
time: 28.4 us; the launch traced here: 28.2 us
  Pallas kernels  27.6 us (97%)
  between operations  0.64 us (2%)
    pallas_call x1, Pallas kernels, per_device(): pl.pallas_call(functools.partial(kernel, back, total), out_shape=[pltpu.V...  26.1 us
    pallas_call x1, Pallas kernels, per_device(): pl.pallas_call(write_out, out_shape=[jax.ShapeDtypeStruct(query.shape, bf...  1.52 us

profile of v9, /device:TPU:0, one launch (start us, length us, event | category | flops | bytes accessed | tf_op | source)
XLA Modules:
  0.0 28.2 jit_solution(6979678319962767100)
XLA Ops:
  0.6 26.1 %shard_map.84 = (bf16[128,4096]{1,0:T(8,128)(2,1)S(1)}, bf16[128,4096]{1,0:T(8,128)(2,1)S(1)}, bf16[128,1024]{1,0:T(8,128)(2,1)S(1)}, bf16[128,1024]{1,0:T(8,128)(2,1)S(1)}) custom-call(s32[32]{0:T(128)} %lens_hbm.1, bf16[128,4096]{1,0:T(8,128)(2,1)} %q_hbm.1, bf16[128,1024]{1,0:T(8,128)(2,1)} %k_hbm.1, bf16[128,1024]{1,0:T(8,128)(2,1)} %v_hbm.1, ...), custom_call_target="tpu_custom_call" | custom-call | tf_op jit(solution)/shard_map/pallas_call | solution.py:338
  26.7 1.5 %shard_map.85 = (bf16[128,4096]{1,0:T(8,128)(2,1)}, bf16[128,4096]{1,0:T(8,128)(2,1)}, bf16[128,1024]{1,0:T(8,128)(2,1)}, bf16[128,1024]{1,0:T(8,128)(2,1)}) custom-call(bf16[128,4096]{1,0:T(8,128)(2,1)S(1)} %get-tuple-element.8.att, bf16[128,4096]{1,0:T(8,128)(2,1)S(1)} %get-tuple-element.9.dq, bf16[128,1024]{1,0:T(8,128)(2,1)S(1)} %get-tuple-element.10.dk, ...), custom_call_target="tpu_custom_call" | custom-call | tf_op jit(solution)/shard_map/pallas_call | solution.py:369
